TPU v7x, 32 devices: a whole 2x2x4 slice. The times are simulated.
32 devices in a mesh: dp: 4 (over x, y), tp: 8 (over z, core).
Axes of the slice: x: 2, y: 2, z: 4, core: 2. Of those that a mesh axis runs over, the one named last changes fastest.
Arguments:
- x: bfloat16 [4096, 8192], P(('dp', 'tp')), parts along dimension 0
- w_gate: bfloat16 [8192, 28672], P(None, 'tp')
- w_up: bfloat16 [8192, 28672], P(None, 'tp')
- w_down: bfloat16 [28672, 8192], P('tp')
Outputs:
- output: bfloat16 [4096, 8192], P(('dp', 'tp')), parts along dimension 0
There are 4 independent parts. A program takes and returns all parts, laid end to end along the dimension named above; an argument that names none is the same for every part.
All inputs are finite; a program needn't handle non-finite values.
Results may differ from a plain program's by a relative error of at most 0.016.
Values are sent between devices in bfloat16 or wider.
A program may use at most 2 GiB of HBM per device.

v0:
```python
import jax
import jax.numpy as jnp
from jax import lax
from jax.sharding import PartitionSpec as P


def solution(mesh):
    def step(x, w_gate, w_up, w_down):
        rows = lax.all_gather(x, "tp", axis=0, tiled=True)
        gate = jnp.dot(rows, w_gate, preferred_element_type=jnp.float32)
        up = jnp.dot(rows, w_up, preferred_element_type=jnp.float32)
        hidden = (jax.nn.silu(gate) * up).astype(jnp.bfloat16)
        term = jnp.dot(hidden, w_down, preferred_element_type=jnp.float32).astype(jnp.bfloat16)
        return lax.psum_scatter(term, "tp", scatter_dimension=0, tiled=True)

    return jax.shard_map(
        step,
        mesh=mesh,
        in_specs=(P(("dp", "tp"), None), P(None, "tp"), P(None, "tp"), P("tp", None)),
        out_specs=P(("dp", "tp"), None),
        check_vma=False,
    )
```

profile of v0, /device:TPU:1, one launch (start us, length us, event | category | flops | bytes accessed | tf_op | source)
XLA Modules:
  0.0 543.8 jit_solution(14994904236264560988)
XLA Ops:
  6.5 0.0 all-gather.2.cloned.1.call-start
  6.5 0.7 all-gather.2.cloned.1.call-update
  7.3 0.0 reduce-scatter.2.cloned.1.call-start
  7.3 155.1 %all-gather.2.cloned.1.call-done = bf16[1024,8192]{1,0:T(8,128)(2,1)} async-done(((bf16[128,8192]{1,0:T(8,128)(2,1)}), bf16[1024,8192]{1,0:T(8,128)(2,1)}) %all-gather.2.cloned.1.call-update) | async-done | bytes 16777232 | tf_op jit(solution)/shard_map/all_gather | solution.py:9
  162.4 71.3 %fusion = f32[1024,3584]{1,0:T(8,128)} fusion(bf16[1024,8192]{1,0:T(8,128)(2,1)} %all-gather.2.cloned.1.call-done, bf16[8192,3584]{1,0:T(8,128)(2,1)} %param.5), kind=kOutput, calls=%fused_computation.2 | convolution fusion | flops 60129542144 | bytes 90177536 | tf_op jit(solution)/shard_map/dot_general | solution.py:10
  233.7 72.1 %multiply_convert_fusion = bf16[1024,3584]{1,0:T(8,128)(2,1)S(1)} fusion(f32[1024,3584]{1,0:T(8,128)} %fusion, bf16[1024,8192]{1,0:T(8,128)(2,1)} %all-gather.2.cloned.1.call-done, bf16[8192,3584]{1,0:T(8,128)(2,1)} %param.6), kind=kOutput, calls=%fused_computation.1 | convolution fusion | flops 60151562240 | bytes 97517568 | tf_op jit(solution)/shard_map/dot_general | solution.py:11
  305.8 66.5 %convolution_convert_fusion = bf16[1024,8192]{1,0:T(8,128)(2,1)} fusion(bf16[1024,3584]{1,0:T(8,128)(2,1)S(1)} %multiply_convert_fusion, bf16[3584,8192]{1,0:T(8,128)(2,1)} %param.7), kind=kOutput, calls=%fused_computation | convolution fusion | flops 60137930752 | bytes 82837504 | tf_op jit(solution)/shard_map/dot_general | solution.py:13
  372.2 0.0 reduce-scatter.2.cloned.1.call-update
  372.3 164.7 %reduce-scatter.2.cloned.1.call-done = bf16[128,8192]{1,0:T(8,128)(2,1)} async-done(((bf16[1024,8192]{1,0:T(8,128)(2,1)}), bf16[128,8192]{1,0:T(8,128)(2,1)}) %reduce-scatter.2.cloned.1.call-update) | async-done | bytes 2097168 | tf_op jit(solution)/shard_map/reduce_scatter | solution.py:14
Async XLA Ops:
  6.5 155.9 %all-gather.2.cloned.1.call-start = ((), (), s32[]{:S(2)}) async-start(), calls=%async_computation.1 | async-start | bytes 18874368 | tf_op jit(solution)/shard_map/all_gather | solution.py:9
  7.3 529.7 %reduce-scatter.2.cloned.1.call-start = ((), (), s32[]{:S(2)}) async-start(), calls=%async_computation.2 | async-start | bytes 18874368 | tf_op jit(solution)/shard_map/reduce_scatter | solution.py:14
Sparse Core Ops, SparseCore 0:
  8.9 153.4 all-gather.1
  372.4 164.5 reduce-scatter.1
where the time goes:
time: 546 us; the launch traced here: 544 us
  waiting for transfers between devices  321 us (59%)
  matrix products  210 us (38%)
  between operations  13.4 us (2%)
    reduce_scatter x1, waiting for transfers between devices, step(): return lax.psum_scatter(term, 'tp', scatter_dimension=0, tiled=True)  165 us
    all_gather x1, waiting for transfers between devices, step(): rows = lax.all_gather(x, 'tp', axis=0, tiled=True)  155 us
    dot_general x1, matrix products, step(): up = jnp.dot(rows, w_up, preferred_element_type=jnp.float32)  72.1 us
    dot_general x1, matrix products, step(): gate = jnp.dot(rows, w_gate, preferred_element_type=jnp.float32)  71.3 us
    dot_general x1, matrix products, step(): jnp.dot(hidden, w_down, preferred_element_type=jnp.float32)  66.5 us
  transfers between devices with their start and end apart: 2, of which 2 were waited for; matrix products, arithmetic and copies ran while one was open for 0% of the time, Pallas kernels for 0%

commit v1 on v0

v1 whole, which is shorter than its diff:
```python
import functools

import jax
import jax.numpy as jnp
from jax import lax
from jax.experimental import pallas as pl
from jax.experimental.pallas import tpu as pltpu
from jax.sharding import PartitionSpec as P

MESH = pl.DeviceIdType.MESH
F32, BF16 = jnp.float32, jnp.bfloat16
PIECES = 8
RING = 3
COMPUTE = 88
LAST = 108
A, B, F, N = 0, 1, 2, 3
IA, IB, OB, IF, IN = 0, 1, 2, 3, 4


def info(t, gj):
    two = 2 * gj
    u = jnp.maximum(t - two, 0)
    span = gj + PIECES
    ph = u // span
    v = u % span
    w = jnp.maximum(v - 4, 0)
    early = t < two
    mid = jnp.logical_and(t >= two, t < two + 2 * span)
    mid_gu = jnp.logical_and(v >= 4, jnp.logical_or(w >= 16, w % 4 != 3))
    is_gu = jnp.logical_or(early, jnp.logical_and(mid, mid_gu))
    i = jnp.where(early, t // gj, 2 + ph)
    j = jnp.where(early, t % gj, jnp.where(w >= 16, w - 4, (w // 4) * 3 + w % 4))
    k = jnp.maximum(t - two - 2 * span, 0)
    st = jnp.where(mid, ph, 2 + k % 2)
    n = jnp.where(mid, jnp.where(v < 4, v, 4 + w // 4), k // 2)
    seq = jnp.where(mid, ph * PIECES + n, 2 * PIECES + k)
    return is_gu, i, j, st, n, seq


def kernel(x_ref, wg_ref, wu_ref, wd_ref, y_ref, xg, wbuf, h, acc, pbuf, sbuf, ybuf, wsem, lsem, ag_p, ag_q, s_q, s_f, s_g,
           p_rx, i_rx, p_tx, s_tx, y_tx, fr_p, f_in, f_out):
    rows, d = x_ref.shape
    hid = wg_ref.shape[1]
    gn = wbuf.shape[-1]
    dn = d // PIECES
    gj = hid // gn
    half = rows // 2

    me = lax.axis_index("tp")
    z, c = me // 2, me % 2
    side = z // 2
    m = (z + side) % 2
    zi = z + 1 - 2 * side
    zo = z - 1 + 2 * side
    partner = {"tp": 2 * z + 1 - c}
    inward = {"tp": 2 * zi + c}
    outward = {"tp": 2 * zo + c}
    end, inner = m == 0, m == 1

    def block(zz, i):
        s = zz // 2
        return jnp.where(i == 0, zz, jnp.where(i == 1, zz + 1 - 2 * (zz % 2), jnp.where(i == 2, 2 - s, 3 - 3 * s)))

    def p_slot(st):
        i = jnp.where(st == A, 0, jnp.where(st == B, 1, jnp.where(st == F, 2, 3)))
        return 2 * block(z, i) + jnp.where(st == F, 1, 0)

    def i_slot(zz, kind):
        i = (0, 1, 2, 3, 0)[kind]
        return 2 * block(zz, i) + (1, 1, 0, 1, 0)[kind]

    def signal(sem, dev):
        pl.semaphore_signal(sem, inc=1, device_id=dev, device_id_type=MESH)

    def remote(src, dst, send, recv, dev):
        return pltpu.make_async_remote_copy(
            src_ref=src, dst_ref=dst, send_sem=send, recv_sem=recv, device_id=dev, device_id_type=MESH
        )

    def loads(t):
        is_gu, _, j, _, n, _ = info(t, gj)
        slot = t % RING
        gc = pl.ds(pl.multiple_of(j * gn, gn), gn)
        gu = [
            pltpu.make_async_copy(wg_ref.at[:, gc], wbuf.at[slot, 0], wsem.at[slot, 0]),
            pltpu.make_async_copy(wu_ref.at[:, gc], wbuf.at[slot, 1], wsem.at[slot, 1]),
        ]
        dd = [
            pltpu.make_async_copy(
                wd_ref.at[:, pl.ds(pl.multiple_of(n * dn + q * gn, gn), gn)],
                wbuf.at[slot, q // 2, pl.ds((q % 2) * hid, hid), :],
                wsem.at[slot, q],
            )
            for q in range(4)
        ]
        return is_gu, gu, dd

    def load(t):
        is_gu, gu, dd = loads(t)

        @pl.when(is_gu)
        def _():
            for cp in gu:
                cp.start()

        @pl.when(jnp.logical_not(is_gu))
        def _():
            for cp in dd:
                cp.start()

    load(jnp.int32(0))
    load(jnp.int32(1))
    own = pltpu.make_async_copy(x_ref, xg.at[me], lsem)
    own.start()

    barrier = pltpu.get_barrier_semaphore()
    signal(barrier, partner)

    @pl.when(z > 0)
    def _():
        signal(barrier, {"tp": me - 2})

    @pl.when(z < 3)
    def _():
        signal(barrier, {"tp": me + 2})

    pl.semaphore_wait(barrier, 3 - jnp.where(m == 0, 1, 0))

    def part(hh):
        return pl.ds(hh * half, half)

    def own_copies(hh):
        src, dst = x_ref.at[part(hh)], xg.at[me, part(hh)]
        return (
            remote(src, dst, s_q.at[z, hh], ag_q.at[z, hh], partner),
            remote(src, dst, s_f.at[z, hh], ag_p.at[z, hh], {"tp": me + 2}),
            remote(src, dst, s_g.at[hh], ag_p.at[z, hh], {"tp": me - 2}),
        )

    def per_way(hh, act):
        q, f, g = own_copies(hh)
        act(q)

        @pl.when(z < 3)
        def _():
            act(f)

        @pl.when(z > 0)
        def _():
            act(g)

    for hh in range(2):
        per_way(hh, lambda cp: cp.start())

    def fwd(o, hh, dev):
        piece = xg.at[2 * o + c, part(hh)]
        return (
            remote(piece, piece, s_q.at[o, hh], ag_q.at[o, hh], partner),
            remote(piece, piece, s_f.at[o, hh], ag_p.at[o, hh], dev),
        )

    def relay(k, hh):
        for sgn in (-1, 1):
            o, nxt = z + sgn * k, z - sgn

            @pl.when(jnp.logical_and(o >= 0, o <= 3))
            def _():
                to_p, on = fwd(o, hh, {"tp": 2 * nxt + c})
                on.wait_recv()
                to_p.start()

                @pl.when(jnp.logical_and(nxt >= 0, nxt <= 3))
                def _():
                    on.start()

    def arrived(o):
        for hh in range(2):
            piece = xg.at[2 * o + 1 - c, part(hh)]
            remote(piece, piece, s_q.at[o, hh], ag_q.at[o, hh], partner).wait_recv()

    def forwarded(o):
        nxt = jnp.where(o > z, z - 1, z + 1)
        for hh in range(2):
            to_p, on = fwd(o, hh, {"tp": 2 * nxt + c})
            to_p.wait_send()

            @pl.when(jnp.logical_and(nxt >= 0, nxt <= 3))
            def _():
                on.wait_send()

    def gate_up(t, i, j):
        b = block(z, i)
        hs = jnp.where(i == 3, 1 - m, i)
        slot = t % RING
        lhs = xg[pl.ds(2 * b, 2)].reshape(2 * rows, d)
        g = jnp.dot(lhs, wbuf[slot, 0], preferred_element_type=F32)
        u = jnp.dot(lhs, wbuf[slot, 1], preferred_element_type=F32)
        v = ((g / (1.0 + jnp.exp(-g))) * u).astype(BF16)
        cols = pl.ds(pl.multiple_of(j * gn, gn), gn)
        h[hs, c, :, cols] = v[:rows]
        h[hs, 1 - c, :, cols] = v[rows:]

    def down(t, st, n, seq):
        slot = t % RING
        hs = jnp.where(st == B, 2, jnp.where(st == N, m, 1 - m))
        ps = seq % 4
        lhs = h[hs].reshape(2 * rows, hid)
        for q in range(4):
            o = jnp.dot(lhs, wbuf[slot, q // 2, (q % 2) * hid:(q % 2 + 1) * hid, :], preferred_element_type=F32)
            acc[st % 2, n, :, q * gn:(q + 1) * gn] = o[:rows]
            pbuf[ps, :, q * gn:(q + 1) * gn] = o[rows:].astype(BF16)

    def cols_of(n):
        return pl.ds(pl.multiple_of(n * dn, dn), dn)

    def to_partner(st, n, seq):
        ps = seq % 4
        return remote(pbuf.at[ps], xg.at[p_slot(st), :, cols_of(n)], p_tx.at[ps], p_rx.at[st, n], partner)

    def incoming(kind, n):
        ref = xg.at[i_slot(z, kind), :, cols_of(n)]
        return ref, remote(ref, ref, s_tx.at[0, 0], i_rx.at[kind, n], inward)

    def chain(way, n, kind):
        dev, zz = (inward, zi) if way == 0 else (outward, zo)
        k = n % 4
        return remote(
            sbuf.at[way, k], xg.at[i_slot(zz, kind), :, cols_of(n)], s_tx.at[way, k], i_rx.at[kind, n], dev
        )

    def both_cores(st, n):
        ref = xg.at[p_slot(st), :, cols_of(n)]
        remote(ref, ref, p_tx.at[0], p_rx.at[st, n], partner).wait_recv()
        return acc[st % 2, n] + ref[...].astype(F32)

    def plus(val, kind, n):
        ref, cp = incoming(kind, n)
        cp.wait_recv()
        return val + ref[...].astype(F32)

    def send_on(st, n, way, kind_in, kind_out, first, free):
        @pl.when(n == 0)
        def _():
            pl.semaphore_wait(free, 1)

        @pl.when(jnp.logical_or(n >= 4, not first))
        def _():
            chain(way, n, kind_out).wait_send()

        val = both_cores(st, n)
        if kind_in is not None:
            val = plus(val, kind_in, n)
        sbuf[way, n % 4] = val.astype(BF16)
        chain(way, n, kind_out).start()

    def y_copy(n):
        return pltpu.make_async_copy(ybuf.at[n % 2], y_ref.at[:, cols_of(n)], y_tx.at[n % 2])

    def finish(val, n):
        @pl.when(n >= 2)
        def _():
            y_copy(n).wait()

        ybuf[n % 2] = val.astype(BF16)
        y_copy(n).start()

    def at(t, start, every, who):
        x = jnp.maximum(t - start, 0)
        hit = jnp.logical_and(jnp.logical_and(t >= start, x < every * PIECES), x % every == 0)
        return x // every, jnp.logical_and(hit, who)

    def step(t, carry):
        @pl.when(t + 2 < COMPUTE)
        def _():
            load(t + 2)

        @pl.when(t == 0)
        def _():
            own.wait()
            arrived(z)

        for when, k, hh in ((11, 1, 0), (14, 1, 1), (24, 2, 0), (32, 2, 1), (42, 3, 0), (54, 3, 1)):
            @pl.when(t == when)
            def _():
                relay(k, hh)

        for when, i in ((14, 1), (32, 2), (54, 3)):
            @pl.when(t == when)
            def _():
                arrived(block(z, i))

        @pl.when(t == 16)
        def _():
            signal(fr_p.at[0], partner)

            @pl.when(inner)
            def _():
                signal(f_in.at[0], outward)

        @pl.when(t == 29)
        def _():
            forwarded(block(z, 1))
            signal(fr_p.at[1], partner)

            @pl.when(inner)
            def _():
                signal(f_in.at[1], outward)

        @pl.when(t == 51)
        def _():
            for hh in range(2):
                per_way(hh, lambda cp: cp.wait_send())
            forwarded(block(z, 2))

            @pl.when(inner)
            def _():
                signal(f_in.at[1], inward)

        @pl.when(t == 58)
        def _():
            @pl.when(inner)
            def _():
                signal(f_in.at[2], inward)

            @pl.when(end)
            def _():
                signal(f_out, inward)

        @pl.when(t == 72)
        def _():
            forwarded(block(z, 3))
            signal(fr_p.at[2], partner)

            @pl.when(inner)
            def _():
                signal(f_in.at[2], outward)

        @pl.when(t < COMPUTE)
        def _():
            is_gu, gu, dd = loads(t)
            _, i, j, st, n, seq = info(t, gj)

            @pl.when(is_gu)
            def _():
                for cp in gu:
                    cp.wait()
                gate_up(t, i, j)

            @pl.when(jnp.logical_not(is_gu))
            def _():
                for cp in dd:
                    cp.wait()

                @pl.when(seq >= 4)
                def _():
                    to_partner(st, n, seq).wait_send()

                down(t, st, n, seq)
                for q in range(3):
                    @pl.when(seq == q * PIECES)
                    def _():
                        pl.semaphore_wait(fr_p.at[q], 1)
                to_partner(st, n, seq).start()

        def event(start, every, who, act):
            n, hit = at(t, start, every, who)

            @pl.when(hit)
            def _():
                act(n)

        event(30, 3, end, lambda n: send_on(A, n, 0, None, IA, True, f_in.at[0]))

        def keep(n):
            acc[0, n] = plus(both_cores(A, n), IA, n)

        event(34, 3, inner, keep)
        event(52, 3, end, lambda n: send_on(B, n, 0, None, IB, False, f_in.at[1]))
        event(56, 3, inner, lambda n: send_on(B, n, 0, IB, OB, True, f_in.at[1]))
        event(60, 3, inner, lambda n: finish(plus(acc[0, n], OB, n), n))
        event(74, 2, end, lambda n: send_on(F, n, 0, None, IF, False, f_in.at[2]))
        event(78, 3, inner, lambda n: send_on(F, n, 0, IF, IN, False, f_in.at[2]))
        event(82, 3, inner, lambda n: send_on(N, n, 1, IN, IN, True, f_out))
        event(86, 3, end, lambda n: finish(plus(both_cores(N, n), IN, n), n))
        return carry

    lax.fori_loop(0, LAST, step, 0)

    for n in (4, 5, 6, 7):
        chain(0, n, IN).wait_send()

        @pl.when(inner)
        def _():
            chain(1, n, IN).wait_send()

        to_partner(N, n, n).wait_send()
    for n in (6, 7):
        y_copy(n).wait()


def mlp(x, w_gate, w_up, w_down, vmem=67043328):
    rows, d = x.shape
    hid = w_gate.shape[1]
    dn = d // PIECES
    gn = dn // 4
    dma, reg = pltpu.SemaphoreType.DMA, pltpu.SemaphoreType.REGULAR
    return pl.pallas_call(
        kernel,
        name="mlp",
        out_shape=jax.ShapeDtypeStruct((rows, d), BF16),
        in_specs=[pl.BlockSpec(memory_space=pl.ANY)] * 4,
        out_specs=pl.BlockSpec(memory_space=pl.ANY),
        scratch_shapes=[
            pltpu.VMEM((8, rows, d), BF16),
            pltpu.VMEM((RING, 2, d, gn), BF16),
            pltpu.VMEM((3, 2, rows, hid), BF16),
            pltpu.VMEM((2, PIECES, rows, dn), F32),
            pltpu.VMEM((4, rows, dn), BF16),
            pltpu.VMEM((2, 4, rows, dn), BF16),
            pltpu.VMEM((2, rows, dn), BF16),
            dma((RING, 4)),
            dma,
            dma((4, 2)),
            dma((4, 2)),
            dma((4, 2)),
            dma((4, 2)),
            dma((2,)),
            dma((4, PIECES)),
            dma((5, PIECES)),
            dma((4,)),
            dma((2, 4)),
            dma((2,)),
            reg((3,)),
            reg((3,)),
            reg,
        ],
        compiler_params=pltpu.CompilerParams(collective_id=0, has_side_effects=True, vmem_limit_bytes=vmem),
    )(x, w_gate, w_up, w_down)


def solution(mesh):
    return jax.shard_map(
        mlp,
        mesh=mesh,
        in_specs=(P(("dp", "tp"), None), P(None, "tp"), P(None, "tp"), P("tp", None)),
        out_specs=P(("dp", "tp"), None),
        check_vma=False,
    )
```

time: 546 us -> 300 us (0.55)
  waiting for transfers between devices: 321 us -> 0 us
  Pallas kernels: 0 us -> 297 us
  matrix products: 210 us -> 0 us
  between operations: 13.4 us -> 0.01 us
    pallas_call x0 -> x1, Pallas kernels: none -> 297 us  [mlp(): pl.pallas_call(kernel, name='mlp', out_shape=jax.ShapeDtypeStruct((rows,...]
    dot_general x3 -> x0, matrix products: 210 us -> none  [the longest x1 72.1 us: step(): up = jnp.dot(rows, w_up, preferred_element_type=jnp.float32)]
    reduce_scatter x1 -> x0, waiting for transfers between devices: 165 us -> none  [step(): return lax.psum_scatter(term, 'tp', scatter_dimension=0, tiled=True)]
    all_gather x1 -> x0, waiting for transfers between devices: 155 us -> none  [step(): rows = lax.all_gather(x, 'tp', axis=0, tiled=True)]
  transfers between devices with their start and end apart: 2 -> 0, of which waited for: 2 -> 0; matrix products, arithmetic and copies ran while one was open for 0% -> 0% of each run, Pallas kernels for 0% -> 0%
where the time goes in v1:
time: 300 us
  Pallas kernels  297 us (99%)
  local copies, waits for them, and re-layouts  3.1 us (1%)
    pallas_call x1, Pallas kernels, mlp(): pl.pallas_call(kernel, name='mlp', out_shape=jax.ShapeDtypeStruct((rows,...  297 us

profile of v1, /device:TPU:1, one launch (start us, length us, event | category | flops | bytes accessed | tf_op | source)
XLA Modules:
  0.0 300.1 jit_solution(9849033489949679388)
XLA Ops:
  0.0 297.0 %mlp.1 = bf16[128,8192]{1,0:T(8,128)(2,1)} custom-call(bf16[128,8192]{1,0:T(8,128)(2,1)} %x_ref.1, bf16[8192,3584]{1,0:T(8,128)(2,1)} %wg_ref.1, bf16[8192,3584]{1,0:T(8,128)(2,1)} %wu_ref.1, bf16[3584,8192]{1,0:T(8,128)(2,1)} %wd_ref.1), custom_call_target="tpu_custom_call" | custom-call | tf_op jit(solution)/shard_map/mlp/pallas_call | solution.py:407
  297.0 3.1 %copy.6 = bf16[128,8192]{1,0:T(8,128)(2,1)} copy(bf16[128,8192]{1,0:T(8,128)(2,1)} %mlp.1) | data formatting | bytes 4194304

commit v2 on v1

--- a/solution.py
+++ b/solution.py
@@ -11,30 +11,40 @@
 F32, BF16 = jnp.float32, jnp.bfloat16
 PIECES = 8
 RING = 3
+PARTS = 4
 COMPUTE = 88
-LAST = 108
+LAST = 102
 A, B, F, N = 0, 1, 2, 3
 IA, IB, OB, IF, IN = 0, 1, 2, 3, 4
 
 
+def div(a, b):
+    return lax.div(jnp.int32(a), jnp.int32(b))
+
+
+def rem(a, b):
+    return lax.rem(jnp.int32(a), jnp.int32(b))
+
+
+def third(t):
+    q = div(t * 171, 512)
+    return q, t - 3 * q
+
+
 def info(t, gj):
-    two = 2 * gj
-    u = jnp.maximum(t - two, 0)
-    span = gj + PIECES
-    ph = u // span
-    v = u % span
-    w = jnp.maximum(v - 4, 0)
-    early = t < two
-    mid = jnp.logical_and(t >= two, t < two + 2 * span)
-    mid_gu = jnp.logical_and(v >= 4, jnp.logical_or(w >= 16, w % 4 != 3))
-    is_gu = jnp.logical_or(early, jnp.logical_and(mid, mid_gu))
-    i = jnp.where(early, t // gj, 2 + ph)
-    j = jnp.where(early, t % gj, jnp.where(w >= 16, w - 4, (w // 4) * 3 + w % 4))
-    k = jnp.maximum(t - two - 2 * span, 0)
-    st = jnp.where(mid, ph, 2 + k % 2)
-    n = jnp.where(mid, jnp.where(v < 4, v, 4 + w // 4), k // 2)
-    seq = jnp.where(mid, ph * PIECES + n, 2 * PIECES + k)
-    return is_gu, i, j, st, n, seq
+    two, span = 2 * gj, gj + PIECES
+    late = jnp.where(t >= gj, 1, 0)
+    ph = jnp.where(t >= two + span, 1, 0)
+    v = t - two - span * ph
+    k = t - two - 2 * span
+    kk = rem(k, 2)
+    early, tail = t < two, k >= 0
+    is_gu = jnp.logical_or(early, jnp.logical_and(v >= PIECES, jnp.logical_not(tail)))
+    i = jnp.where(early, late, 2 + ph)
+    j = jnp.where(early, t - gj * late, v - PIECES)
+    st = jnp.where(tail, 2 + kk, ph)
+    n = jnp.where(tail, div(k, 2), v)
+    return is_gu, i, j, st, n, jnp.where(tail, 2 * PIECES + k, PIECES * ph + n)
 
 
 def kernel(x_ref, wg_ref, wu_ref, wd_ref, y_ref, xg, wbuf, h, acc, pbuf, sbuf, ybuf, wsem, lsem, ag_p, ag_q, s_q, s_f, s_g,
@@ -47,9 +57,9 @@
     half = rows // 2
 
     me = lax.axis_index("tp")
-    z, c = me // 2, me % 2
-    side = z // 2
-    m = (z + side) % 2
+    z, c = div(me, 2), rem(me, 2)
+    side = div(z, 2)
+    m = rem(z + side, 2)
     zi = z + 1 - 2 * side
     zo = z - 1 + 2 * side
     partner = {"tp": 2 * z + 1 - c}
@@ -58,8 +68,8 @@
     end, inner = m == 0, m == 1
 
     def block(zz, i):
-        s = zz // 2
-        return jnp.where(i == 0, zz, jnp.where(i == 1, zz + 1 - 2 * (zz % 2), jnp.where(i == 2, 2 - s, 3 - 3 * s)))
+        s = div(zz, 2)
+        return jnp.where(i == 0, zz, jnp.where(i == 1, zz + 1 - 2 * rem(zz, 2), jnp.where(i == 2, 2 - s, 3 - 3 * s)))
 
     def p_slot(st):
         i = jnp.where(st == A, 0, jnp.where(st == B, 1, jnp.where(st == F, 2, 3)))
@@ -79,7 +89,7 @@
 
     def loads(t):
         is_gu, _, j, _, n, _ = info(t, gj)
-        slot = t % RING
+        slot = third(t)[1]
         gc = pl.ds(pl.multiple_of(j * gn, gn), gn)
         gu = [
             pltpu.make_async_copy(wg_ref.at[:, gc], wbuf.at[slot, 0], wsem.at[slot, 0]),
@@ -191,7 +201,7 @@
     def gate_up(t, i, j):
         b = block(z, i)
         hs = jnp.where(i == 3, 1 - m, i)
-        slot = t % RING
+        slot = third(t)[1]
         lhs = xg[pl.ds(2 * b, 2)].reshape(2 * rows, d)
         g = jnp.dot(lhs, wbuf[slot, 0], preferred_element_type=F32)
         u = jnp.dot(lhs, wbuf[slot, 1], preferred_element_type=F32)
@@ -201,139 +211,162 @@
         h[hs, 1 - c, :, cols] = v[rows:]
 
     def down(t, st, n, seq):
-        slot = t % RING
+        slot = third(t)[1]
         hs = jnp.where(st == B, 2, jnp.where(st == N, m, 1 - m))
-        ps = seq % 4
+        ps = rem(seq, 4)
         lhs = h[hs].reshape(2 * rows, hid)
         for q in range(4):
             o = jnp.dot(lhs, wbuf[slot, q // 2, (q % 2) * hid:(q % 2 + 1) * hid, :], preferred_element_type=F32)
-            acc[st % 2, n, :, q * gn:(q + 1) * gn] = o[:rows]
+            acc[rem(st, 2), n, :, q * gn:(q + 1) * gn] = o[:rows]
             pbuf[ps, :, q * gn:(q + 1) * gn] = o[rows:].astype(BF16)
 
     def cols_of(n):
         return pl.ds(pl.multiple_of(n * dn, dn), dn)
 
     def to_partner(st, n, seq):
-        ps = seq % 4
+        ps = rem(seq, 4)
         return remote(pbuf.at[ps], xg.at[p_slot(st), :, cols_of(n)], p_tx.at[ps], p_rx.at[st, n], partner)
 
-    def incoming(kind, n):
-        ref = xg.at[i_slot(z, kind), :, cols_of(n)]
-        return ref, remote(ref, ref, s_tx.at[0, 0], i_rx.at[kind, n], inward)
-
-    def chain(way, n, kind):
+    hc = dn // PARTS
+
+    def half_of(n, e):
+        return pl.ds(pl.multiple_of(n * dn + e * hc, hc), hc)
+
+    def incoming(kind, n, e):
+        ref = xg.at[i_slot(z, kind), :, half_of(n, e)]
+        return ref, remote(ref, ref, s_tx.at[0, 0, 0], i_rx.at[kind, n, e], inward)
+
+    def chain(way, n, e, kind):
         dev, zz = (inward, zi) if way == 0 else (outward, zo)
-        k = n % 4
+        k = rem(n, 4)
         return remote(
-            sbuf.at[way, k], xg.at[i_slot(zz, kind), :, cols_of(n)], s_tx.at[way, k], i_rx.at[kind, n], dev
+            sbuf.at[way, k, e], xg.at[i_slot(zz, kind), :, half_of(n, e)], s_tx.at[way, k, e], i_rx.at[kind, n, e], dev
         )
 
-    def both_cores(st, n):
+    def from_partner(st, n):
         ref = xg.at[p_slot(st), :, cols_of(n)]
         remote(ref, ref, p_tx.at[0], p_rx.at[st, n], partner).wait_recv()
-        return acc[st % 2, n] + ref[...].astype(F32)
-
-    def plus(val, kind, n):
-        ref, cp = incoming(kind, n)
+
+    def both_cores(st, n, e):
+        return acc[rem(st, 2), n, :, pl.ds(pl.multiple_of(e * hc, hc), hc)] + xg[p_slot(st), :, half_of(n, e)].astype(F32)
+
+    def plus(val, kind, n, e):
+        ref, cp = incoming(kind, n, e)
         cp.wait_recv()
         return val + ref[...].astype(F32)
 
+    def ready(st, n, free):
+        @pl.when(n == 0)
+        def _():
+            pl.semaphore_wait(free, 1)
+
+        from_partner(st, n)
+
+    def send_part(st, n, e, way, kind_in, kind_out, first):
+        @pl.when(jnp.logical_or(n >= 4, not first))
+        def _():
+            chain(way, n, e, kind_out).wait_send()
+
+        val = both_cores(st, n, e)
+        if kind_in is not None:
+            val = plus(val, kind_in, n, e)
+        sbuf[way, rem(n, 4), e] = val.astype(BF16)
+        chain(way, n, e, kind_out).start()
+
     def send_on(st, n, way, kind_in, kind_out, first, free):
-        @pl.when(n == 0)
-        def _():
-            pl.semaphore_wait(free, 1)
-
-        @pl.when(jnp.logical_or(n >= 4, not first))
-        def _():
-            chain(way, n, kind_out).wait_send()
-
-        val = both_cores(st, n)
-        if kind_in is not None:
-            val = plus(val, kind_in, n)
-        sbuf[way, n % 4] = val.astype(BF16)
-        chain(way, n, kind_out).start()
+        ready(st, n, free)
+        for e in range(PARTS):
+            send_part(st, n, e, way, kind_in, kind_out, first)
 
     def y_copy(n):
-        return pltpu.make_async_copy(ybuf.at[n % 2], y_ref.at[:, cols_of(n)], y_tx.at[n % 2])
+        k = rem(n, 2)
+        return pltpu.make_async_copy(ybuf.at[k], y_ref.at[:, cols_of(n)], y_tx.at[k])
 
     def finish(val, n):
         @pl.when(n >= 2)
         def _():
             y_copy(n).wait()
 
-        ybuf[n % 2] = val.astype(BF16)
+        for e in range(PARTS):
+            ybuf[rem(n, 2), :, e * hc:(e + 1) * hc] = val(e).astype(BF16)
         y_copy(n).start()
 
     def at(t, start, every, who):
-        x = jnp.maximum(t - start, 0)
-        hit = jnp.logical_and(jnp.logical_and(t >= start, x < every * PIECES), x % every == 0)
-        return x // every, jnp.logical_and(hit, who)
+        x = 2 * (t - start)
+        n = div(x, 4) if every == 4 else div(x * 205, 1024)
+        r = x - every * n
+        hit = jnp.logical_and(jnp.logical_and(x >= 0, n < PIECES), r < 2)
+        return n, jnp.logical_and(hit, who)
 
     def step(t, carry):
         @pl.when(t + 2 < COMPUTE)
         def _():
             load(t + 2)
 
-        @pl.when(t == 0)
-        def _():
-            own.wait()
-            arrived(z)
-
-        for when, k, hh in ((11, 1, 0), (14, 1, 1), (24, 2, 0), (32, 2, 1), (42, 3, 0), (54, 3, 1)):
-            @pl.when(t == when)
-            def _():
-                relay(k, hh)
-
-        for when, i in ((14, 1), (32, 2), (54, 3)):
-            @pl.when(t == when)
-            def _():
-                arrived(block(z, i))
-
-        @pl.when(t == 16)
-        def _():
-            signal(fr_p.at[0], partner)
-
-            @pl.when(inner)
-            def _():
-                signal(f_in.at[0], outward)
-
-        @pl.when(t == 29)
-        def _():
-            forwarded(block(z, 1))
-            signal(fr_p.at[1], partner)
-
-            @pl.when(inner)
-            def _():
-                signal(f_in.at[1], outward)
-
-        @pl.when(t == 51)
-        def _():
-            for hh in range(2):
-                per_way(hh, lambda cp: cp.wait_send())
-            forwarded(block(z, 2))
-
-            @pl.when(inner)
-            def _():
-                signal(f_in.at[1], inward)
-
-        @pl.when(t == 58)
-        def _():
-            @pl.when(inner)
-            def _():
-                signal(f_in.at[2], inward)
-
-            @pl.when(end)
-            def _():
-                signal(f_out, inward)
-
-        @pl.when(t == 72)
-        def _():
-            forwarded(block(z, 3))
-            signal(fr_p.at[2], partner)
-
-            @pl.when(inner)
-            def _():
-                signal(f_in.at[2], outward)
+        some = functools.reduce(jnp.logical_or, [t == w for w in (0, 13, 14, 16, 25, 34, 36, 44, 45, 51, 55, 58, 72)])
+
+        @pl.when(some)
+        def _():
+            @pl.when(t == 0)
+            def _():
+                own.wait()
+                arrived(z)
+
+            for when, k, hh in ((13, 1, 0), (14, 1, 1), (25, 2, 0), (34, 2, 1), (45, 3, 0), (55, 3, 1)):
+                @pl.when(t == when)
+                def _():
+                    relay(k, hh)
+
+            for when, i in ((14, 1), (36, 2), (58, 3)):
+                @pl.when(t == when)
+                def _():
+                    arrived(block(z, i))
+
+            @pl.when(t == 16)
+            def _():
+                signal(fr_p.at[0], partner)
+
+                @pl.when(inner)
+                def _():
+                    signal(f_in.at[0], outward)
+
+            @pl.when(t == 44)
+            def _():
+                forwarded(block(z, 1))
+                signal(fr_p.at[1], partner)
+
+                @pl.when(inner)
+                def _():
+                    signal(f_in.at[1], outward)
+
+            @pl.when(t == 51)
+            def _():
+                for hh in range(2):
+                    per_way(hh, lambda cp: cp.wait_send())
+                forwarded(block(z, 2))
+
+                @pl.when(inner)
+                def _():
+                    signal(f_in.at[1], inward)
+
+            @pl.when(t == 58)
+            def _():
+                @pl.when(inner)
+                def _():
+                    signal(f_in.at[2], inward)
+
+                @pl.when(end)
+                def _():
+                    signal(f_out, inward)
+
+            @pl.when(t == 72)
+            def _():
+                forwarded(block(z, 3))
+                signal(fr_p.at[2], partner)
+
+                @pl.when(inner)
+                def _():
+                    signal(f_in.at[2], outward)
 
         @pl.when(t < COMPUTE)
         def _():
@@ -362,6 +395,31 @@
                         pl.semaphore_wait(fr_p.at[q], 1)
                 to_partner(st, n, seq).start()
 
+        def keep(n):
+            from_partner(A, n)
+            for e in range(PARTS):
+                acc[0, n, :, e * hc:(e + 1) * hc] = plus(both_cores(A, n, e), IA, n, e)
+
+        def last(n):
+            from_partner(N, n)
+            finish(lambda e: plus(both_cores(N, n, e), IN, n, e), n)
+
+        def pieces():
+            for b in range(2):
+                for st, way, kind, free, g in (
+                    (F, 0, IF, f_in.at[2], 2 * (t - 75) + b),
+                    (N, 1, IN, f_out, 2 * (t - 75) + b - PARTS),
+                ):
+                    n, e = div(g, PARTS), rem(g, PARTS)
+
+                    @pl.when(jnp.logical_and(g >= 0, g < PARTS * PIECES))
+                    def _():
+                        @pl.when(e == 0)
+                        def _():
+                            ready(st, n, free)
+
+                        send_part(st, n, e, way, kind, IN, st == N)
+
         def event(start, every, who, act):
             n, hit = at(t, start, every, who)
 
@@ -369,29 +427,38 @@
             def _():
                 act(n)
 
-        event(30, 3, end, lambda n: send_on(A, n, 0, None, IA, True, f_in.at[0]))
-
-        def keep(n):
-            acc[0, n] = plus(both_cores(A, n), IA, n)
-
-        event(34, 3, inner, keep)
-        event(52, 3, end, lambda n: send_on(B, n, 0, None, IB, False, f_in.at[1]))
-        event(56, 3, inner, lambda n: send_on(B, n, 0, IB, OB, True, f_in.at[1]))
-        event(60, 3, inner, lambda n: finish(plus(acc[0, n], OB, n), n))
-        event(74, 2, end, lambda n: send_on(F, n, 0, None, IF, False, f_in.at[2]))
-        event(78, 3, inner, lambda n: send_on(F, n, 0, IF, IN, False, f_in.at[2]))
-        event(82, 3, inner, lambda n: send_on(N, n, 1, IN, IN, True, f_out))
-        event(86, 3, end, lambda n: finish(plus(both_cores(N, n), IN, n), n))
+        @pl.when(jnp.logical_and(t >= 30, t < 56))
+        def _():
+            event(30, 4, end, lambda n: send_on(A, n, 0, None, IA, True, f_in.at[0]))
+            event(34, 5, inner, keep)
+
+        @pl.when(jnp.logical_and(t >= 52, t < 80))
+        def _():
+            event(52, 4, end, lambda n: send_on(B, n, 0, None, IB, False, f_in.at[1]))
+            event(56, 5, inner, lambda n: send_on(B, n, 0, IB, OB, True, f_in.at[1]))
+            event(60, 5, inner, lambda n: finish(lambda e: plus(acc[0, n, :, e * hc:(e + 1) * hc], OB, n, e), n))
+
+        @pl.when(t >= 73)
+        def _():
+            event(73, 4, end, lambda n: send_on(F, n, 0, None, IF, False, f_in.at[2]))
+            event(83, 5, end, last)
+
+            @pl.when(jnp.logical_and(t >= 75, inner))
+            def _():
+                pieces()
+
         return carry
 
     lax.fori_loop(0, LAST, step, 0)
 
     for n in (4, 5, 6, 7):
-        chain(0, n, IN).wait_send()
+        for e in range(PARTS):
+            chain(0, n, e, IN).wait_send()
 
         @pl.when(inner)
         def _():
-            chain(1, n, IN).wait_send()
+            for e in range(PARTS):
+                chain(1, n, e, IN).wait_send()
 
         to_partner(N, n, n).wait_send()
     for n in (6, 7):
@@ -416,7 +483,7 @@
             pltpu.VMEM((3, 2, rows, hid), BF16),
             pltpu.VMEM((2, PIECES, rows, dn), F32),
             pltpu.VMEM((4, rows, dn), BF16),
-            pltpu.VMEM((2, 4, rows, dn), BF16),
+            pltpu.VMEM((2, 4, PARTS, rows, dn // PARTS), BF16),
             pltpu.VMEM((2, rows, dn), BF16),
             dma((RING, 4)),
             dma,
@@ -426,9 +493,9 @@
             dma((4, 2)),
             dma((2,)),
             dma((4, PIECES)),
-            dma((5, PIECES)),
+            dma((5, PIECES, PARTS)),
             dma((4,)),
-            dma((2, 4)),
+            dma((2, 4, PARTS)),
             dma((2,)),
             reg((3,)),
             reg((3,)),

time: 300 us -> 266 us (0.89)
  Pallas kernels: 297 us -> 263 us
    pallas_call x1, Pallas kernels: 297 us -> 263 us  [mlp(): pl.pallas_call(kernel, name='mlp', out_shape=jax.ShapeDtypeStruct((rows,...]
where the time goes in v2:
time: 266 us
  Pallas kernels  263 us (99%)
  local copies, waits for them, and re-layouts  3.1 us (1%)
    pallas_call x1, Pallas kernels, mlp(): pl.pallas_call(kernel, name='mlp', out_shape=jax.ShapeDtypeStruct((rows,...  263 us

profile of v2, /device:TPU:1, one launch (start us, length us, event | category | flops | bytes accessed | tf_op | source)
XLA Modules:
  0.0 265.9 jit_solution(16577405471374448647)
XLA Ops:
  0.0 262.8 %mlp.1 = bf16[128,8192]{1,0:T(8,128)(2,1)} custom-call(bf16[128,8192]{1,0:T(8,128)(2,1)} %x_ref.1, bf16[8192,3584]{1,0:T(8,128)(2,1)} %wg_ref.1, bf16[8192,3584]{1,0:T(8,128)(2,1)} %wu_ref.1, bf16[3584,8192]{1,0:T(8,128)(2,1)} %wd_ref.1), custom_call_target="tpu_custom_call" | custom-call | tf_op jit(solution)/shard_map/mlp/pallas_call | solution.py:474
  262.8 3.1 %copy.6 = bf16[128,8192]{1,0:T(8,128)(2,1)} copy(bf16[128,8192]{1,0:T(8,128)(2,1)} %mlp.1) | data formatting | bytes 4194304

commit v3 on v2

--- a/solution.py
+++ b/solution.py
@@ -27,27 +27,31 @@
 
 
 def third(t):
-    q = div(t * 171, 512)
-    return q, t - 3 * q
-
-
-def info(t, gj):
-    two, span = 2 * gj, gj + PIECES
-    late = jnp.where(t >= gj, 1, 0)
-    ph = jnp.where(t >= two + span, 1, 0)
-    v = t - two - span * ph
-    k = t - two - 2 * span
-    kk = rem(k, 2)
-    early, tail = t < two, k >= 0
-    is_gu = jnp.logical_or(early, jnp.logical_and(v >= PIECES, jnp.logical_not(tail)))
-    i = jnp.where(early, late, 2 + ph)
-    j = jnp.where(early, t - gj * late, v - PIECES)
-    st = jnp.where(tail, 2 + kk, ph)
-    n = jnp.where(tail, div(k, 2), v)
-    return is_gu, i, j, st, n, jnp.where(tail, 2 * PIECES + k, PIECES * ph + n)
-
-
-def kernel(x_ref, wg_ref, wu_ref, wd_ref, y_ref, xg, wbuf, h, acc, pbuf, sbuf, ybuf, wsem, lsem, ag_p, ag_q, s_q, s_f, s_g,
+    return t - 3 * div(t * 171, 512)
+
+
+def parity(st):
+    return st % 2 if isinstance(st, int) else rem(st, 2)
+
+
+def passes(gj):
+    out, t = [], 0
+    for gu, what in ((True, 0), (True, 1), (False, (A,)), (True, 2), (False, (B,)), (True, 3), (False, (F, N))):
+        end = t + (gj if gu else PIECES * len(what))
+        out.append((t, end, gu, what))
+        t = end
+    return out
+
+
+def place(t, lo, what):
+    k = t - lo
+    if len(what) == 1:
+        return what[0], k, PIECES * what[0] + k
+    q = rem(k, 2)
+    return what[0] + q, div(k, 2), PIECES * what[0] + k
+
+
+def kernel(x_ref, wg_ref, wu_ref, wd_ref, y_ref, xg, wbuf, h, gs, us, acc, pbuf, sbuf, ybuf, wsem, lsem, ag_p, ag_q, s_q, s_f, s_g,
            p_rx, i_rx, p_tx, s_tx, y_tx, fr_p, f_in, f_out):
     rows, d = x_ref.shape
     hid = wg_ref.shape[1]
@@ -69,11 +73,12 @@
 
     def block(zz, i):
         s = div(zz, 2)
-        return jnp.where(i == 0, zz, jnp.where(i == 1, zz + 1 - 2 * rem(zz, 2), jnp.where(i == 2, 2 - s, 3 - 3 * s)))
+        return (zz, zz + 1 - 2 * rem(zz, 2), 2 - s, 3 - 3 * s)[i]
 
     def p_slot(st):
-        i = jnp.where(st == A, 0, jnp.where(st == B, 1, jnp.where(st == F, 2, 3)))
-        return 2 * block(z, i) + jnp.where(st == F, 1, 0)
+        if isinstance(st, int):
+            return 2 * block(z, st) + (1 if st == F else 0)
+        return jnp.where(st == F, p_slot(F), p_slot(N))
 
     def i_slot(zz, kind):
         i = (0, 1, 2, 3, 0)[kind]
@@ -87,15 +92,19 @@
             src_ref=src, dst_ref=dst, send_sem=send, recv_sem=recv, device_id=dev, device_id_type=MESH
         )
 
-    def loads(t):
-        is_gu, _, j, _, n, _ = info(t, gj)
-        slot = third(t)[1]
-        gc = pl.ds(pl.multiple_of(j * gn, gn), gn)
-        gu = [
-            pltpu.make_async_copy(wg_ref.at[:, gc], wbuf.at[slot, 0], wsem.at[slot, 0]),
-            pltpu.make_async_copy(wu_ref.at[:, gc], wbuf.at[slot, 1], wsem.at[slot, 1]),
-        ]
-        dd = [
+    segments = passes(gj)
+
+    def copies(t, seg):
+        lo, _, gu, what = seg
+        slot = third(t)
+        if gu:
+            gc = pl.ds(pl.multiple_of((t - lo) * gn, gn), gn)
+            return [
+                pltpu.make_async_copy(wg_ref.at[:, gc], wbuf.at[slot, 0], wsem.at[slot, 0]),
+                pltpu.make_async_copy(wu_ref.at[:, gc], wbuf.at[slot, 1], wsem.at[slot, 1]),
+            ]
+        _, n, _ = place(t, lo, what)
+        return [
             pltpu.make_async_copy(
                 wd_ref.at[:, pl.ds(pl.multiple_of(n * dn + q * gn, gn), gn)],
                 wbuf.at[slot, q // 2, pl.ds((q % 2) * hid, hid), :],
@@ -103,23 +112,13 @@
             )
             for q in range(4)
         ]
-        return is_gu, gu, dd
-
-    def load(t):
-        is_gu, gu, dd = loads(t)
-
-        @pl.when(is_gu)
-        def _():
-            for cp in gu:
-                cp.start()
-
-        @pl.when(jnp.logical_not(is_gu))
-        def _():
-            for cp in dd:
-                cp.start()
-
-    load(jnp.int32(0))
-    load(jnp.int32(1))
+
+    def load(t, seg):
+        for cp in copies(t, seg):
+            cp.start()
+
+    load(jnp.int32(0), segments[0])
+    load(jnp.int32(1), segments[0])
     own = pltpu.make_async_copy(x_ref, xg.at[me], lsem)
     own.start()
 
@@ -198,26 +197,36 @@
             def _():
                 on.wait_send()
 
-    def gate_up(t, i, j):
-        b = block(z, i)
-        hs = jnp.where(i == 3, 1 - m, i)
-        slot = third(t)[1]
-        lhs = xg[pl.ds(2 * b, 2)].reshape(2 * rows, d)
-        g = jnp.dot(lhs, wbuf[slot, 0], preferred_element_type=F32)
-        u = jnp.dot(lhs, wbuf[slot, 1], preferred_element_type=F32)
+    def hidden(hs, j):
+        g, u = gs[...], us[...]
         v = ((g / (1.0 + jnp.exp(-g))) * u).astype(BF16)
         cols = pl.ds(pl.multiple_of(j * gn, gn), gn)
         h[hs, c, :, cols] = v[:rows]
         h[hs, 1 - c, :, cols] = v[rows:]
 
+    def gate_up(t, i, j):
+        b = block(z, i)
+        hs = 1 - m if i == 3 else i
+        slot = third(t)
+        hidden(hs, jnp.maximum(j - 1, 0))
+        lhs = xg[pl.ds(2 * b, 2)].reshape(2 * rows, d)
+        g = jnp.dot(lhs, wbuf[slot, 0], preferred_element_type=F32)
+        u = jnp.dot(lhs, wbuf[slot, 1], preferred_element_type=F32)
+        gs[...] = g
+        us[...] = u
+
+        @pl.when(j == gj - 1)
+        def _():
+            hidden(hs, j)
+
     def down(t, st, n, seq):
-        slot = third(t)[1]
-        hs = jnp.where(st == B, 2, jnp.where(st == N, m, 1 - m))
+        slot = third(t)
+        hs = (1 - m, 2)[st] if isinstance(st, int) else jnp.where(st == N, m, 1 - m)
         ps = rem(seq, 4)
         lhs = h[hs].reshape(2 * rows, hid)
         for q in range(4):
             o = jnp.dot(lhs, wbuf[slot, q // 2, (q % 2) * hid:(q % 2 + 1) * hid, :], preferred_element_type=F32)
-            acc[rem(st, 2), n, :, q * gn:(q + 1) * gn] = o[:rows]
+            acc[parity(st), n, :, q * gn:(q + 1) * gn] = o[:rows]
             pbuf[ps, :, q * gn:(q + 1) * gn] = o[rows:].astype(BF16)
 
     def cols_of(n):
@@ -248,7 +257,7 @@
         remote(ref, ref, p_tx.at[0], p_rx.at[st, n], partner).wait_recv()
 
     def both_cores(st, n, e):
-        return acc[rem(st, 2), n, :, pl.ds(pl.multiple_of(e * hc, hc), hc)] + xg[p_slot(st), :, half_of(n, e)].astype(F32)
+        return acc[parity(st), n, :, pl.ds(pl.multiple_of(e * hc, hc), hc)] + xg[p_slot(st), :, half_of(n, e)].astype(F32)
 
     def plus(val, kind, n, e):
         ref, cp = incoming(kind, n, e)
@@ -298,102 +307,88 @@
         hit = jnp.logical_and(jnp.logical_and(x >= 0, n < PIECES), r < 2)
         return n, jnp.logical_and(hit, who)
 
-    def step(t, carry):
-        @pl.when(t + 2 < COMPUTE)
-        def _():
-            load(t + 2)
-
-        some = functools.reduce(jnp.logical_or, [t == w for w in (0, 13, 14, 16, 25, 34, 36, 44, 45, 51, 55, 58, 72)])
-
-        @pl.when(some)
-        def _():
-            @pl.when(t == 0)
-            def _():
-                own.wait()
-                arrived(z)
-
-            for when, k, hh in ((13, 1, 0), (14, 1, 1), (25, 2, 0), (34, 2, 1), (45, 3, 0), (55, 3, 1)):
-                @pl.when(t == when)
+    def handoff(i):
+        if i > 0:
+            forwarded(block(z, i))
+        if i == 2:
+            for hh in range(2):
+                per_way(hh, lambda cp: cp.wait_send())
+        else:
+            signal(fr_p.at[(0, 1, None, 2)[i]], partner)
+
+        @pl.when(inner)
+        def _():
+            if i == 2:
+                signal(f_in.at[1], inward)
+            else:
+                signal(f_in.at[(0, 1, None, 2)[i]], outward)
+
+    def first_rows():
+        own.wait()
+        arrived(z)
+
+    def again():
+        @pl.when(inner)
+        def _():
+            signal(f_in.at[2], inward)
+
+        @pl.when(end)
+        def _():
+            signal(f_out, inward)
+
+    once = (
+        (0, first_rows),
+        (13, lambda: relay(1, 0)),
+        (14, lambda: relay(1, 1)),
+        (14, lambda: arrived(block(z, 1))),
+        (16, lambda: handoff(0)),
+        (25, lambda: relay(2, 0)),
+        (34, lambda: relay(2, 1)),
+        (36, lambda: arrived(block(z, 2))),
+        (44, lambda: handoff(1)),
+        (45, lambda: relay(3, 0)),
+        (51, lambda: handoff(2)),
+        (55, lambda: relay(3, 1)),
+        (58, lambda: arrived(block(z, 3))),
+        (58, again),
+        (72, lambda: handoff(3)),
+    )
+
+    def step(seg, nxt, t, carry):
+        lo, hi, gu, what = seg
+        if gu is not None:
+            @pl.when(t + 2 < hi)
+            def _():
+                load(t + 2, seg)
+
+            if nxt is not None and nxt[2] is not None:
+                @pl.when(t + 2 >= hi)
                 def _():
-                    relay(k, hh)
-
-            for when, i in ((14, 1), (36, 2), (58, 3)):
-                @pl.when(t == when)
-                def _():
-                    arrived(block(z, i))
-
-            @pl.when(t == 16)
-            def _():
-                signal(fr_p.at[0], partner)
-
-                @pl.when(inner)
-                def _():
-                    signal(f_in.at[0], outward)
-
-            @pl.when(t == 44)
-            def _():
-                forwarded(block(z, 1))
-                signal(fr_p.at[1], partner)
-
-                @pl.when(inner)
-                def _():
-                    signal(f_in.at[1], outward)
-
-            @pl.when(t == 51)
-            def _():
-                for hh in range(2):
-                    per_way(hh, lambda cp: cp.wait_send())
-                forwarded(block(z, 2))
-
-                @pl.when(inner)
-                def _():
-                    signal(f_in.at[1], inward)
-
-            @pl.when(t == 58)
-            def _():
-                @pl.when(inner)
-                def _():
-                    signal(f_in.at[2], inward)
-
-                @pl.when(end)
-                def _():
-                    signal(f_out, inward)
-
-            @pl.when(t == 72)
-            def _():
-                forwarded(block(z, 3))
-                signal(fr_p.at[2], partner)
-
-                @pl.when(inner)
-                def _():
-                    signal(f_in.at[2], outward)
-
-        @pl.when(t < COMPUTE)
-        def _():
-            is_gu, gu, dd = loads(t)
-            _, i, j, st, n, seq = info(t, gj)
-
-            @pl.when(is_gu)
-            def _():
-                for cp in gu:
-                    cp.wait()
-                gate_up(t, i, j)
-
-            @pl.when(jnp.logical_not(is_gu))
-            def _():
-                for cp in dd:
-                    cp.wait()
-
-                @pl.when(seq >= 4)
-                def _():
-                    to_partner(st, n, seq).wait_send()
-
-                down(t, st, n, seq)
-                for q in range(3):
-                    @pl.when(seq == q * PIECES)
-                    def _():
-                        pl.semaphore_wait(fr_p.at[q], 1)
-                to_partner(st, n, seq).start()
+                    load(t + 2, nxt)
+
+        for when, act in once:
+            if lo <= when < hi:
+                pl.when(t == when)(act)
+
+        if gu is not None:
+            for cp in copies(t, seg):
+                cp.wait()
+        if gu:
+            gate_up(t, what, t - lo)
+        elif gu is False:
+            st, n, seq = place(t, lo, what)
+
+            @pl.when(seq >= 4)
+            def _():
+                to_partner(st, n, seq).wait_send()
+
+            down(t, st, n, seq)
+
+            @pl.when(t == lo)
+            def _():
+                pl.semaphore_wait(fr_p.at[what[0]], 1)
+
+            to_partner(st, n, seq).start()
 
         def keep(n):
             from_partner(A, n)
@@ -421,35 +416,31 @@
                         send_part(st, n, e, way, kind, IN, st == N)
 
         def event(start, every, who, act):
+            if start >= hi or start + (every * (PIECES - 1) + 1) // 2 < lo:
+                return
             n, hit = at(t, start, every, who)
 
             @pl.when(hit)
             def _():
                 act(n)
 
-        @pl.when(jnp.logical_and(t >= 30, t < 56))
-        def _():
-            event(30, 4, end, lambda n: send_on(A, n, 0, None, IA, True, f_in.at[0]))
-            event(34, 5, inner, keep)
-
-        @pl.when(jnp.logical_and(t >= 52, t < 80))
-        def _():
-            event(52, 4, end, lambda n: send_on(B, n, 0, None, IB, False, f_in.at[1]))
-            event(56, 5, inner, lambda n: send_on(B, n, 0, IB, OB, True, f_in.at[1]))
-            event(60, 5, inner, lambda n: finish(lambda e: plus(acc[0, n, :, e * hc:(e + 1) * hc], OB, n, e), n))
-
-        @pl.when(t >= 73)
-        def _():
-            event(73, 4, end, lambda n: send_on(F, n, 0, None, IF, False, f_in.at[2]))
-            event(83, 5, end, last)
-
+        event(30, 4, end, lambda n: send_on(A, n, 0, None, IA, True, f_in.at[0]))
+        event(34, 5, inner, keep)
+        event(52, 4, end, lambda n: send_on(B, n, 0, None, IB, False, f_in.at[1]))
+        event(56, 5, inner, lambda n: send_on(B, n, 0, IB, OB, True, f_in.at[1]))
+        event(60, 5, inner, lambda n: finish(lambda e: plus(acc[0, n, :, e * hc:(e + 1) * hc], OB, n, e), n))
+        event(73, 4, end, lambda n: send_on(F, n, 0, None, IF, False, f_in.at[2]))
+        event(83, 5, end, last)
+        if hi > 75:
             @pl.when(jnp.logical_and(t >= 75, inner))
             def _():
                 pieces()
 
         return carry
 
-    lax.fori_loop(0, LAST, step, 0)
+    segments = segments + [(COMPUTE, LAST, None, None)]
+    for seg, nxt in zip(segments, segments[1:] + [None]):
+        lax.fori_loop(seg[0], seg[1], functools.partial(step, seg, nxt), 0)
 
     for n in (4, 5, 6, 7):
         for e in range(PARTS):
@@ -481,6 +472,8 @@
             pltpu.VMEM((8, rows, d), BF16),
             pltpu.VMEM((RING, 2, d, gn), BF16),
             pltpu.VMEM((3, 2, rows, hid), BF16),
+            pltpu.VMEM((2 * rows, gn), F32),
+            pltpu.VMEM((2 * rows, gn), F32),
             pltpu.VMEM((2, PIECES, rows, dn), F32),
             pltpu.VMEM((4, rows, dn), BF16),
             pltpu.VMEM((2, 4, PARTS, rows, dn // PARTS), BF16),

time: 266 us -> 262 us (0.985)
  Pallas kernels: 263 us -> 259 us
    pallas_call x1, Pallas kernels: 263 us -> 259 us  [mlp(): pl.pallas_call(kernel, name='mlp', out_shape=jax.ShapeDtypeStruct((rows,...]
where the time goes in v3:
time: 262 us
  Pallas kernels  259 us (99%)
  local copies, waits for them, and re-layouts  3.1 us (1%)
    pallas_call x1, Pallas kernels, mlp(): pl.pallas_call(kernel, name='mlp', out_shape=jax.ShapeDtypeStruct((rows,...  259 us

profile of v3, /device:TPU:1, one launch (start us, length us, event | category | flops | bytes accessed | tf_op | source)
XLA Modules:
  0.0 261.9 jit_solution(4520768366200905219)
XLA Ops:
  0.0 258.8 %mlp.1 = bf16[128,8192]{1,0:T(8,128)(2,1)} custom-call(bf16[128,8192]{1,0:T(8,128)(2,1)} %x_ref.1, bf16[8192,3584]{1,0:T(8,128)(2,1)} %wg_ref.1, bf16[8192,3584]{1,0:T(8,128)(2,1)} %wu_ref.1, bf16[3584,8192]{1,0:T(8,128)(2,1)} %wd_ref.1), custom_call_target="tpu_custom_call" | custom-call | tf_op jit(solution)/shard_map/mlp/pallas_call | solution.py:465
  258.8 3.1 %copy.6 = bf16[128,8192]{1,0:T(8,128)(2,1)} copy(bf16[128,8192]{1,0:T(8,128)(2,1)} %mlp.1) | data formatting | bytes 4194304
